TPU v7x, 128 devices: a whole 4x4x4 slice. The times are simulated.
128 devices in a mesh: gx: 4 (over y), gy: 4 (over z_hi, core), gz: 8 (over z_lo, x).
Axes of the slice: x: 4, y: 4, z: 4 (z_hi: 2, z_lo: 2; z = z_hi * 2 + z_lo), core: 2. Of those that a mesh axis runs over, the one named last changes fastest.
Arguments:
- volume: bfloat16 [32, 32, 32, 32, 128], P('gx', 'gy', 'gz'), may hold values from -6 to 6
- conv_kernel: bfloat16 [3, 3, 3, 32, 64], replicated, may hold values from -0.21875 to 0.21875
- dense_one: bfloat16 [16, 16, 16, 64, 2048], P('gx', None, None, ('gy', 'gz')), may hold values from -0.01171875 to 0.01171875
- dense_two: float32 [2048, 256], replicated, may hold values from -0.125 to 0.125
- dense_three: float32 [256, 4], replicated, may hold values from -0.375 to 0.375
- targets: float32 [4, 128], replicated, may hold values from -3 to 3
Outputs:
- prediction: float32 [4, 128], replicated
- grad_dense_one: bfloat16 [16, 16, 16, 64, 2048], P('gx', None, None, ('gy', 'gz'))
- grad_conv: float32 [3, 3, 3, 32, 64], replicated
- grad_volume: bfloat16 [32, 32, 32, 32, 128], P('gx', 'gy', 'gz')
All inputs are finite; a program needn't handle non-finite values.
Results may differ from a plain program's by a relative error of at most 0.008.
Values may be sent and summed in bfloat16 or wider, within the bound.
A program may use at most 128 MiB of HBM per device.

v0:
```python
import jax
import jax.numpy as jnp
from jax import lax
from jax.sharding import PartitionSpec as P

loss_scale = 1024.0
leak_slope = 0.3


def with_halo(array, sides, width):
    for axis, dim in sides:
        size, length = (lax.axis_size(axis), array.shape[dim])
        up = [(i, (i + 1) % size) for i in range(size - 1)]
        down = [(j, i) for i, j in up]
        last = lax.slice_in_dim(array, length - width, length, axis=dim)
        initial = lax.slice_in_dim(array, 0, width, axis=dim)
        before = lax.ppermute(last, axis, up)
        after = lax.ppermute(initial, axis, down)
        array = jnp.concatenate([before, array, after], axis=dim)
    return array


def from_behind(block, axis, distance):
    devices = range(lax.axis_size(axis))
    route = [(i - distance, i) for i in devices if i - distance in devices]
    return lax.ppermute(block, axis, route)


def shortened(array):
    return jax.tree.map(lambda a: a.astype(jnp.bfloat16) if a.dtype == jnp.float32 else a, array)


def smooth_leaky(values):
    return leak_slope * values + (1.0 - leak_slope) * jax.nn.softplus(values)


def leaky_derivative(values):
    return leak_slope + (1.0 - leak_slope) * jax.nn.sigmoid(values)


def conv_forward(padded, kernel):
    return lax.conv_general_dilated(
        padded,
        kernel,
        (1, 1, 1),
        "VALID",
        dimension_numbers=("DHWCN", "DHWIO", "DHWCN"),
        preferred_element_type=jnp.float32,
    )


def conv_back_input(padded_grad, kernel):
    flipped = kernel[::-1, ::-1, ::-1]
    return lax.conv_general_dilated(
        padded_grad,
        flipped,
        (1, 1, 1),
        "VALID",
        dimension_numbers=("DHWCN", "DHWOI", "DHWCN"),
        preferred_element_type=jnp.float32,
    )


def conv_back_kernel(padded, gradient):
    return lax.conv_general_dilated(
        padded,
        gradient,
        (1, 1, 1),
        "VALID",
        dimension_numbers=("DHWNC", "DHWOI", "DHWNC"),
        preferred_element_type=jnp.float32,
    )


def pooling(values):
    extent_x, extent_y, extent_z, channels, samples = values.shape
    return values.reshape(
        extent_x // 2, 2, extent_y // 2, 2, extent_z // 2, 2, channels, samples
    ).mean(axis=(1, 3, 5))


def spread(values):
    extent_x, extent_y, extent_z, channels, samples = values.shape
    widened = jnp.broadcast_to(
        values[:, None, :, None, :, None],
        (extent_x, 2, extent_y, 2, extent_z, 2, channels, samples),
    )
    return widened.reshape(2 * extent_x, 2 * extent_y, 2 * extent_z, channels, samples)


def fold_faces(inner, from_below, from_above, axis_dim):
    length = inner.shape[axis_dim]
    first = lax.slice_in_dim(inner, 0, 1, axis=axis_dim) + from_below
    middle = lax.slice_in_dim(inner, 1, length - 1, axis=axis_dim)
    last = lax.slice_in_dim(inner, length - 1, length, axis=axis_dim) + from_above
    return jnp.concatenate([first, middle, last], axis=axis_dim)


def body(volume, conv_kernel, dense_one, dense_two, dense_three, targets):
    padded = with_halo(volume, (("gx", 0), ("gy", 1), ("gz", 2)), 1)
    conv_out = conv_forward(padded, conv_kernel)
    pooled = pooling(smooth_leaky(conv_out)).astype(jnp.bfloat16)
    half_x, half_y, half_z, channels, samples = pooled.shape
    groups_y = lax.axis_size("gy")
    groups_z = lax.axis_size("gz")
    per_group = channels // (groups_y * groups_z)
    arrived = lax.all_to_all(pooled[None], ("gy", "gz"), split_axis=4, concat_axis=0, tiled=True)
    arrived = arrived.reshape(groups_y, groups_z, half_x, half_y, half_z, per_group, samples)
    weights_local = dense_one.reshape(
        half_x, groups_y, half_y, groups_z, half_z, per_group, dense_one.shape[4]
    )
    partial_one = jnp.einsum(
        "uvxyzcb,xuyvzch->hb", arrived, weights_local, preferred_element_type=jnp.float32
    )
    pre_one = lax.psum(partial_one, ("gx", "gy", "gz"))
    hidden_one = smooth_leaky(pre_one)
    pre_two = jnp.dot(dense_two.T, hidden_one, precision=lax.Precision.HIGHEST)
    hidden_two = smooth_leaky(pre_two)
    prediction = jnp.dot(dense_three.T, hidden_two, precision=lax.Precision.HIGHEST)
    error_grad = loss_scale * (prediction - targets)
    grad_pre_two = jnp.dot(
        dense_three, error_grad, precision=lax.Precision.HIGHEST
    ) * leaky_derivative(pre_two)
    grad_pre_one = (
        jnp.dot(dense_two, grad_pre_two, precision=lax.Precision.HIGHEST)
        * leaky_derivative(pre_one)
    ).astype(jnp.bfloat16)
    grad_local = jnp.einsum(
        "uvxyzcb,hb->xuyvzch", arrived, grad_pre_one, preferred_element_type=jnp.float32
    )
    grad_dense_one = (grad_local / samples).astype(jnp.bfloat16).reshape(dense_one.shape)
    grad_arrived = jnp.einsum(
        "xuyvzch,hb->uvxyzcb", weights_local, grad_pre_one, preferred_element_type=jnp.float32
    ).astype(jnp.bfloat16)
    outgoing = grad_arrived.reshape(groups_y * groups_z, half_x, half_y, half_z, per_group, samples)
    returned = lax.all_to_all(outgoing, ("gy", "gz"), split_axis=0, concat_axis=4, tiled=True)
    grad_pooled = returned.reshape(half_x, half_y, half_z, channels, samples)
    grad_out = (spread(grad_pooled.astype(jnp.float32)) / 8.0 * leaky_derivative(conv_out)).astype(
        jnp.bfloat16
    )
    widened = jnp.pad(grad_out, ((2, 2), (2, 2), (2, 2), (0, 0), (0, 0)))
    whole = conv_back_input(widened, conv_kernel)
    below_x = from_behind(whole[-1:].astype(jnp.bfloat16), "gx", 1).astype(jnp.float32)
    above_x = from_behind(whole[:1].astype(jnp.bfloat16), "gx", -1).astype(jnp.float32)
    folded = fold_faces(whole[1:-1], below_x, above_x, 0)
    below_y = from_behind(shortened(folded[:, -1:]), "gy", 1)
    above_y = from_behind(shortened(folded[:, :1]), "gy", -1)
    folded = fold_faces(folded[:, 1:-1], below_y, above_y, 1)
    below_z = from_behind(shortened(folded[:, :, -1:]), "gz", 1)
    above_z = from_behind(shortened(folded[:, :, :1]), "gz", -1)
    folded = fold_faces(folded[:, :, 1:-1], below_z, above_z, 2)
    grad_volume = folded.astype(jnp.bfloat16)
    kernel_local = conv_back_kernel(padded, grad_out)
    grad_conv = lax.psum(kernel_local, ("gx", "gy", "gz")) / samples
    return (prediction, grad_dense_one, grad_conv, grad_volume)


def solution(mesh):
    return jax.shard_map(
        body,
        mesh=mesh,
        in_specs=(
            P("gx", "gy", "gz", None, None),
            P(),
            P("gx", None, None, ("gy", "gz"), None),
            P(),
            P(),
            P(),
        ),
        out_specs=(
            P(),
            P("gx", None, None, ("gy", "gz"), None),
            P(),
            P("gx", "gy", "gz", None, None),
        ),
        check_vma=False,
    )
```

profile of v0, /device:TPU:1, one launch (start us, length us, event | category | flops | bytes accessed | tf_op | source)
XLA Modules:
  0.0 538.4 jit_solution(12310446413016146924)
XLA Ops:
  7.2 1.2 fusion.69
  8.4 4.0 collective-permute-start
  12.5 1.3 collective-permute-start.1
  13.8 3.7 collective-permute-done
  17.5 2.4 constant_dynamic-update-slice_fusion.1
  19.9 1.4 collective-permute-done.1
  21.4 7.2 %collective-permute-start.2 = (bf16[10,1,4,32,128]{4,3,2,1,0:T(8,128)(2,1)S(1)}, bf16[10,1,4,32,128]{4,3,2,1,0:T(8,128)(2,1)S(1)}, u32[]{:S(2)}, u32[]{:S(2)}) collective-permute-start(bf16[10,1,4,32,128]{4,3,2,1,0:T(8,128)(2,1)S(1)} %get-tuple-element.18), channel_id=1, source_target_pairs={{0,8},{8,16},{16,24},{1,9},{9,17},{17,25},{2,10},{10,18},{18,26},{... | collective-permute-start | bytes 983048 | tf_op jit(solution)/shard_map/ppermute | solution.py:17
  28.6 1.9 collective-permute-start.3
  30.5 2.1 collective-permute-done.2
  32.6 23.5 %collective-permute-done.3 = bf16[10,1,4,32,128]{4,3,2,1,0:T(8,128)(2,1)S(1)} collective-permute-done((bf16[10,1,4,32,128]{4,3,2,1,0:T(8,128)(2,1)S(1)}, bf16[10,1,4,32,128]{4,3,2,1,0:T(8,128)(2,1)S(1)}, u32[]{:S(2)}, u32[]{:S(2)}) %collective-permute-start.3) | collective-permute-done | bytes 327712 | tf_op jit(solution)/shard_map/ppermute | solution.py:18
  56.3 1.3 collective-permute-start.4
  57.6 1.3 collective-permute-start.5
  58.9 7.9 %collective-permute-done.4 = bf16[10,10,1,32,128]{4,3,2,1,0:T(8,128)(2,1)S(1)} collective-permute-done((bf16[10,10,1,32,128]{4,3,2,1,0:T(8,128)(2,1)S(1)}, bf16[10,10,1,32,128]{4,3,2,1,0:T(8,128)(2,1)S(1)}, u32[]{:S(2)}, u32[]{:S(2)}) %collective-permute-start.4) | collective-permute-done | bytes 819232 | tf_op jit(solution)/shard_map/ppermute | solution.py:17
  66.8 3.9 collective-permute-done.5
  70.7 18.1 %fusion.2 = (f32[8,8,4,64,128]{4,3,2,1,0:T(8,128)}, f32[8,8,4,64,128]{4,3,2,1,0:T(8,128)}) fusion(bf16[3,3,3,32,64]{4,3,2,1,0:T(8,128)(2,1)S(1)} %copy-done.12, bf16[10,10,1,32,128]{4,3,2,1,0:T(8,128)(2,1)S(1)} %collective-permute-done.5, bf16[10,1,4,32,128]{4,3,2,1,0:T(8,128)(2,1)S(1)} %collective-permute-done.3, ...), kind=kOutput, calls=%fused_computation.4 | convolution fusion | flops 3652583424 | bytes 21803008 | tf_op jit(solution)/shard_map/conv_general_dilated | solution.py:42
  88.8 4.4 reduce_sum.9
  93.9 13.4 %all_to_all.24 = bf16[1,4,4,2,64,128]{5,3,2,1,0,4:T(2,128)(2,1)S(1)} all-to-all(bf16[1,4,4,2,64,128]{5,3,2,1,0,4:T(2,128)(2,1)S(1)} %copy.45), channel_id=1, replica_groups=mesh['gx'=4,'gy'=4,'gz'=8] {'gy','gz'}, dimensions={4} | all-to-all | bytes 1048576 | tf_op jit(solution)/shard_map/all_to_all | solution.py:107
  107.6 13.7 %fusion.7 = f32[2048,128]{0,1:T(8,128)} fusion(bf16[4,4,4,8,2,2,2048]{6,5,4,3,2,1,0:T(2,128)(2,1)} %bitcast.72, bf16[32,1,4,4,2,2,128]{6,5,0,4,3,2,1:T(2,128)(2,1)S(1)} %bitcast.70), kind=kOutput, calls=%fused_computation.14 | convolution fusion | flops 1073741824 | bytes 9961472 | tf_op jit(solution)/shard_map/uvxyzcb,xuyvzch->hb/dot_general | solution.py:112
  121.6 145.5 %all-reduce.3.cloned.1.call-done = f32[2048,128]{0,1:T(8,128)} async-done(((f32[2048,128]{0,1:T(8,128)}), f32[2048,128]{0,1:T(8,128)}) %all-reduce.3.cloned.1.call-update) | async-done | bytes 1048592 | tf_op jit(solution)/shard_map/psum | solution.py:115
  267.1 3.0 convolution_bitcast_fusion.2
  270.7 3.5 fusion.12
  274.3 8.6 %fusion.16 = bf16[4,8,4,4,2,2,128]{6,1,5,4,3,0,2:T(8,128)(2,1)S(1)} fusion(bf16[2048,128,1,1,1,1,1]{0,1,6,5,4,3,2:T(8,128)(2,1)S(1)} %fusion.12, bf16[4,4,4,8,2,2,2048]{6,5,4,3,2,1,0:T(2,128)(2,1)} %bitcast.73), kind=kOutput, calls=%fused_computation.21 | convolution fusion | flops 1074003968 | bytes 9437184 | tf_op jit(solution)/shard_map/xuyvzch,hb->uvxyzcb/dot_general | solution.py:132
  283.6 17.6 %all_to_all.25 = bf16[32,4,4,2,2,128]{5,4,3,2,1,0:T(2,128)(2,1)S(1)} all-to-all(bf16[32,4,4,2,2,128]{5,4,3,2,1,0:T(2,128)(2,1)S(1)} %copy.56), channel_id=1, replica_groups=mesh['gx'=4,'gy'=4,'gz'=8] {'gy','gz'}, dimensions={0} | all-to-all | bytes 1048576 | tf_op jit(solution)/shard_map/all_to_all | solution.py:136
  302.3 1.1 broadcast_in_dim.2
  303.4 1.1 slice-done.2
  304.5 2.8 multiply_convert_fusion.1
  307.3 29.9 %fusion.70 = (bf16[10,10,6,32,128]{4,3,2,1,0:T(8,128)(2,1)S(1)}, f32[10,10,6,32,128]{4,3,2,1,0:T(8,128)S(1)}) fusion(bf16[8,8,4,64,128]{4,3,2,1,0:T(8,128)(2,1)S(1)} %multiply_convert_fusion.1, bf16[3,3,3,32,64]{4,3,2,1,0:T(8,128)(2,1)S(1)} %copy-done.13), kind=kOutput, calls=%fused_computation.92 | convolution fusion | flops 3626336256 | bytes 19050496 | tf_op jit(solution)/shard_map/conv_general_dilated | solution.py:54
  337.3 2.0 collective-permute-start.6
  339.3 1.3 collective-permute-start.7
  340.6 1.2 slice.107
  341.8 7.6 %collective-permute-done.6 = bf16[1,10,6,32,128]{4,3,2,1,0:T(8,128)(2,1)S(1)} collective-permute-done((bf16[1,10,6,32,128]{4,3,2,1,0:T(8,128)(2,1)S(1)}, bf16[1,10,6,32,128]{4,3,2,1,0:T(8,128)(2,1)S(1)}, u32[]{:S(2)}, u32[]{:S(2)}) %collective-permute-start.6) | collective-permute-done | bytes 491552 | tf_op jit(solution)/shard_map/ppermute | solution.py:26
  349.4 3.9 collective-permute-done.7
  353.7 0.6 fusion.64
  354.4 4.0 collective-permute-start.8
  358.4 2.1 collective-permute-start.9
  360.6 15.5 %fusion.61 = f32[3,3,3,32,64]{4,3,2,1,0:T(8,128)} fusion(bf16[8,8,4,64,128]{4,3,2,1,0:T(8,128)(2,1)S(1)} %multiply_convert_fusion.1, bf16[10,10,1,32,128]{4,3,2,1,0:T(8,128)(2,1)S(1)} %copy-done.17, bf16[10,1,4,32,128]{4,3,2,1,0:T(8,128)(2,1)S(1)} %copy-done.11, bf16[10,8,4,32,128]{4,3,2,1,0:T(8,128)(2,1)S(1)} %copy-done.7, ...), kind=kOutput, calls=%fused_computation.83 | convolution fusion | flops 3633709056 | bytes 9330688 | tf_op jit(solution)/shard_map/conv_general_dilated | solution.py:65
  376.1 3.5 pad_maximum_fusion
  380.1 2.0 slice_add_fusion.5
  382.6 1.2 fusion.67
  383.9 3.0 collective-permute-start.10
  386.8 1.5 collective-permute-start.11
  388.3 2.3 fusion
  390.7 9.4 %copy.52 = bf16[4,4,4,8,2,2,2048]{6,5,4,3,2,1,0:T(2,128)(2,1)} copy(bf16[4,4,4,8,2,2,2048]{6,3,5,4,2,0,1:T(8,128)(2,1)S(1)} %fusion) | data formatting | bytes 16777216 | tf_op jit(solution)/shard_map/convert_element_type | solution.py:131
  400.0 122.7 %all-reduce.5.cloned.1.call-done = f32[3,3,3,32,64]{4,3,2,1,0:T(8,128)} async-done(((f32[3,3,3,32,64]{4,3,2,1,0:T(8,128)}), f32[3,3,3,32,64]{4,3,2,1,0:T(8,128)}) %all-reduce.5.cloned.1.call-update) | async-done | bytes 221200 | tf_op jit(solution)/shard_map/psum | solution.py:154
  522.8 1.8 broadcast_multiply_fusion
  524.6 3.4 pad_maximum_fusion.1
  528.1 1.7 fusion.24
  529.7 1.5 pad_maximum_fusion.3
  (78 shorter events, 5.5 us)
Async XLA Ops:
  7.2 259.9 %copy-start = (f32[2048,256]{1,0:T(8,128)S(1)}, f32[2048,256]{1,0:T(8,128)}, u32[]{:S(2)}) copy-start(f32[2048,256]{1,0:T(8,128)} %param.9) | copy-start | bytes 6291460
  7.2 259.9 %all-reduce.3.cloned.1.call-start = ((), (), s32[]{:S(2)}) async-start(), calls=%async_computation.2 | async-start | bytes 2097152 | tf_op jit(solution)/shard_map/psum | solution.py:115
  8.4 9.0 %collective-permute-start = (bf16[1,8,4,32,128]{4,3,2,1,0:T(8,128)(2,1)S(1)}, bf16[1,8,4,32,128]{4,3,2,1,0:T(8,128)(2,1)S(1)}, u32[]{:S(2)}, u32[]{:S(2)}) collective-permute-start(bf16[1,8,4,32,128]{4,3,2,1,0:T(8,128)(2,1)S(1)} %get-tuple-element.21), channel_id=1, source_target_pairs={{0,32},{32,64},{64,96},{1,33},{33,65},{65,97},{2,34},{34,66},{66,9... | collective-permute-start | bytes 786440 | tf_op jit(solution)/shard_map/ppermute | solution.py:17
  12.5 8.8 %collective-permute-start.1 = (bf16[1,8,4,32,128]{4,3,2,1,0:T(8,128)(2,1)S(1)}, bf16[1,8,4,32,128]{4,3,2,1,0:T(8,128)(2,1)S(1)}, u32[]{:S(2)}, u32[]{:S(2)}) collective-permute-start(bf16[1,8,4,32,128]{4,3,2,1,0:T(8,128)(2,1)S(1)} %get-tuple-element.20), channel_id=1, source_target_pairs={{32,0},{64,32},{96,64},{33,1},{65,33},{97,65},{34,2},{66,34},{98,6... | collective-permute-start | bytes 786440 | tf_op jit(solution)/shard_map/ppermute | solution.py:18
  17.5 53.2 %copy-start.12 = (bf16[3,3,3,32,64]{4,3,2,1,0:T(8,128)(2,1)S(1)}, bf16[3,3,3,32,64]{4,3,2,1,0:T(8,128)(2,1)}, u32[]{:S(2)}) copy-start(bf16[3,3,3,32,64]{4,3,2,1,0:T(8,128)(2,1)} %param.7) | copy-start | bytes 331780
  21.3 67.4 %copy-start.6 = (bf16[10,8,4,32,128]{4,3,2,1,0:T(8,128)(2,1)}, bf16[10,8,4,32,128]{4,3,2,1,0:T(8,128)(2,1)S(1)}, u32[]{:S(2)}) copy-start(bf16[10,8,4,32,128]{4,3,2,1,0:T(8,128)(2,1)S(1)} %constant_dynamic-update-slice_fusion) | copy-start | bytes 7864324
  21.4 11.2 %collective-permute-start.2 = (bf16[10,1,4,32,128]{4,3,2,1,0:T(8,128)(2,1)S(1)}, bf16[10,1,4,32,128]{4,3,2,1,0:T(8,128)(2,1)S(1)}, u32[]{:S(2)}, u32[]{:S(2)}) collective-permute-start(bf16[10,1,4,32,128]{4,3,2,1,0:T(8,128)(2,1)S(1)} %get-tuple-element.18), channel_id=1, source_target_pairs={{0,8},{8,16},{16,24},{1,9},{9,17},{17,25},{2,10},{10,18},{18,26},{... | collective-permute-start | bytes 983048 | tf_op jit(solution)/shard_map/ppermute | solution.py:17
  28.6 27.5 %collective-permute-start.3 = (bf16[10,1,4,32,128]{4,3,2,1,0:T(8,128)(2,1)S(1)}, bf16[10,1,4,32,128]{4,3,2,1,0:T(8,128)(2,1)S(1)}, u32[]{:S(2)}, u32[]{:S(2)}) collective-permute-start(bf16[10,1,4,32,128]{4,3,2,1,0:T(8,128)(2,1)S(1)} %get-tuple-element.19), channel_id=1, source_target_pairs={{8,0},{16,8},{24,16},{9,1},{17,9},{25,17},{10,2},{18,10},{26,18},{... | collective-permute-start | bytes 983048 | tf_op jit(solution)/shard_map/ppermute | solution.py:18
  32.6 56.2 %copy-start.8 = (bf16[10,1,4,32,128]{4,3,2,1,0:T(8,128)(2,1)}, bf16[10,1,4,32,128]{4,3,2,1,0:T(8,128)(2,1)S(1)}, u32[]{:S(2)}) copy-start(bf16[10,1,4,32,128]{4,3,2,1,0:T(8,128)(2,1)S(1)} %collective-permute-done.2) | copy-start | bytes 983044
  56.1 32.7 %copy-start.10 = (bf16[10,1,4,32,128]{4,3,2,1,0:T(8,128)(2,1)}, bf16[10,1,4,32,128]{4,3,2,1,0:T(8,128)(2,1)S(1)}, u32[]{:S(2)}) copy-start(bf16[10,1,4,32,128]{4,3,2,1,0:T(8,128)(2,1)S(1)} %collective-permute-done.3) | copy-start | bytes 983044
  56.3 10.6 %collective-permute-start.4 = (bf16[10,10,1,32,128]{4,3,2,1,0:T(8,128)(2,1)S(1)}, bf16[10,10,1,32,128]{4,3,2,1,0:T(8,128)(2,1)S(1)}, u32[]{:S(2)}, u32[]{:S(2)}) collective-permute-start(bf16[10,10,1,32,128]{4,3,2,1,0:T(8,128)(2,1)S(1)} %get-tuple-element.14), channel_id=1, source_target_pairs={{0,1},{1,2},{2,3},{3,4},{4,5},{5,6},{6,7},{8,9},{9,10},{10,11},{11... | collective-permute-start | bytes 2457608 | tf_op jit(solution)/shard_map/ppermute | solution.py:17
  57.6 13.1 %collective-permute-start.5 = (bf16[10,10,1,32,128]{4,3,2,1,0:T(8,128)(2,1)S(1)}, bf16[10,10,1,32,128]{4,3,2,1,0:T(8,128)(2,1)S(1)}, u32[]{:S(2)}, u32[]{:S(2)}) collective-permute-start(bf16[10,10,1,32,128]{4,3,2,1,0:T(8,128)(2,1)S(1)} %get-tuple-element.15), channel_id=1, source_target_pairs={{1,0},{2,1},{3,2},{4,3},{5,4},{6,5},{7,6},{9,8},{10,9},{11,10},{12... | collective-permute-start | bytes 2457608 | tf_op jit(solution)/shard_map/ppermute | solution.py:18
  66.8 22.0 %copy-start.14 = (bf16[10,10,1,32,128]{4,3,2,1,0:T(8,128)(2,1)}, bf16[10,10,1,32,128]{4,3,2,1,0:T(8,128)(2,1)S(1)}, u32[]{:S(2)}) copy-start(bf16[10,10,1,32,128]{4,3,2,1,0:T(8,128)(2,1)S(1)} %collective-permute-done.4) | copy-start | bytes 2457604
  70.7 18.1 %copy-start.16 = (bf16[10,10,1,32,128]{4,3,2,1,0:T(8,128)(2,1)}, bf16[10,10,1,32,128]{4,3,2,1,0:T(8,128)(2,1)S(1)}, u32[]{:S(2)}) copy-start(bf16[10,10,1,32,128]{4,3,2,1,0:T(8,128)(2,1)S(1)} %collective-permute-done.5) | copy-start | bytes 2457604
  107.5 162.5 %copy-start.18 = (f32[256,4]{0,1:T(4,128)S(1)}, f32[256,4]{0,1:T(4,128)}, u32[]{:S(2)}) copy-start(f32[256,4]{0,1:T(4,128)} %param.10) | copy-start | bytes 12292
  107.6 162.8 %copy-start.19 = (f32[4,128]{1,0:T(4,128)S(1)}, f32[4,128]{1,0:T(4,128)}, u32[]{:S(2)}) copy-start(f32[4,128]{1,0:T(4,128)} %param.11) | copy-start | bytes 6148
  121.3 401.4 %all-reduce.5.cloned.1.call-start = ((), (), s32[]{:S(2)}) async-start(), calls=%async_computation.3 | async-start | bytes 884736 | tf_op jit(solution)/shard_map/psum | solution.py:154
  270.3 12.5 %copy-start.20 = (f32[4,128]{1,0:T(4,128)}, f32[4,128]{1,0:T(4,128)S(1)}, u32[]{:S(2)}) copy-start(f32[4,128]{1,0:T(4,128)S(1)} %convolution_bitcast_fusion.3) | copy-start | bytes 6148
  274.3 8.6 %copy-start.21 = (bf16[2048,128,1,1,1,1,1]{0,1,6,5,4,3,2:T(8,128)(2,1)}, bf16[2048,128,1,1,1,1,1]{0,1,6,5,4,3,2:T(8,128)(2,1)S(1)}, u32[]{:S(2)}) copy-start(bf16[2048,128,1,1,1,1,1]{0,1,6,5,4,3,2:T(8,128)(2,1)S(1)} %fusion.12) | copy-start | bytes 1572868
  283.0 20.3 %slice-start.1 = ((s8[8388608]{0:T(1024)(128)(4,1)}), s8[4194304]{0:T(1024)(128)(4,1)S(1)}, s32[]{:S(2)}) async-start(s8[8388608]{0:T(1024)(128)(4,1)} %bitcast.65), calls=%async_computation.5 | async-start | bytes 8388608
  302.3 2.2 slice-start.2
  304.5 2.8 copy-start.13
  337.3 12.2 %collective-permute-start.6 = (bf16[1,10,6,32,128]{4,3,2,1,0:T(8,128)(2,1)S(1)}, bf16[1,10,6,32,128]{4,3,2,1,0:T(8,128)(2,1)S(1)}, u32[]{:S(2)}, u32[]{:S(2)}) collective-permute-start(bf16[1,10,6,32,128]{4,3,2,1,0:T(8,128)(2,1)S(1)} %get-tuple-element.10), channel_id=1, source_target_pairs={{0,32},{32,64},{64,96},{1,33},{33,65},{65,97},{2,34},{34,66},{66,9... | collective-permute-start | bytes 1474568 | tf_op jit(solution)/shard_map/ppermute | solution.py:26
  339.3 14.0 %collective-permute-start.7 = (bf16[1,10,6,32,128]{4,3,2,1,0:T(8,128)(2,1)S(1)}, bf16[1,10,6,32,128]{4,3,2,1,0:T(8,128)(2,1)S(1)}, u32[]{:S(2)}, u32[]{:S(2)}) collective-permute-start(bf16[1,10,6,32,128]{4,3,2,1,0:T(8,128)(2,1)S(1)} %get-tuple-element.11), channel_id=1, source_target_pairs={{32,0},{64,32},{96,64},{33,1},{65,33},{97,65},{34,2},{66,34},{98,6... | collective-permute-start | bytes 1474568 | tf_op jit(solution)/shard_map/ppermute | solution.py:26
  341.8 12.5 %copy-start.2 = (f32[6,10,6,32,128]{4,3,2,1,0:T(8,128)}, f32[6,10,6,32,128]{4,3,2,1,0:T(8,128)S(1)}, u32[]{:S(2)}) copy-start(f32[6,10,6,32,128]{4,3,2,1,0:T(8,128)S(1)} %slice.107) | copy-start | bytes 17694724
  353.6 6.9 %copy-start.7 = (bf16[10,8,4,32,128]{4,3,2,1,0:T(8,128)(2,1)S(1)}, bf16[10,8,4,32,128]{4,3,2,1,0:T(8,128)(2,1)}, u32[]{:S(2)}) copy-start(bf16[10,8,4,32,128]{4,3,2,1,0:T(8,128)(2,1)} %copy-done.6) | copy-start | bytes 7864324
  353.6 6.9 %copy-start.9 = (bf16[10,1,4,32,128]{4,3,2,1,0:T(8,128)(2,1)S(1)}, bf16[10,1,4,32,128]{4,3,2,1,0:T(8,128)(2,1)}, u32[]{:S(2)}) copy-start(bf16[10,1,4,32,128]{4,3,2,1,0:T(8,128)(2,1)} %copy-done.8) | copy-start | bytes 983044
  353.6 6.9 %copy-start.11 = (bf16[10,1,4,32,128]{4,3,2,1,0:T(8,128)(2,1)S(1)}, bf16[10,1,4,32,128]{4,3,2,1,0:T(8,128)(2,1)}, u32[]{:S(2)}) copy-start(bf16[10,1,4,32,128]{4,3,2,1,0:T(8,128)(2,1)} %copy-done.10) | copy-start | bytes 983044
  353.7 6.9 %copy-start.15 = (bf16[10,10,1,32,128]{4,3,2,1,0:T(8,128)(2,1)S(1)}, bf16[10,10,1,32,128]{4,3,2,1,0:T(8,128)(2,1)}, u32[]{:S(2)}) copy-start(bf16[10,10,1,32,128]{4,3,2,1,0:T(8,128)(2,1)} %copy-done.14) | copy-start | bytes 2457604
  353.7 6.9 %copy-start.17 = (bf16[10,10,1,32,128]{4,3,2,1,0:T(8,128)(2,1)S(1)}, bf16[10,10,1,32,128]{4,3,2,1,0:T(8,128)(2,1)}, u32[]{:S(2)}) copy-start(bf16[10,10,1,32,128]{4,3,2,1,0:T(8,128)(2,1)} %copy-done.16) | copy-start | bytes 2457604
  354.4 25.7 %collective-permute-start.8 = (bf16[8,1,6,32,128]{4,3,2,1,0:T(8,128)(2,1)S(1)}, bf16[8,1,6,32,128]{4,3,2,1,0:T(8,128)(2,1)}, u32[]{:S(2)}, u32[]{:S(2)}) collective-permute-start(bf16[8,1,6,32,128]{4,3,2,1,0:T(8,128)(2,1)S(1)} %get-tuple-element.12), channel_id=1, source_target_pairs={{0,8},{8,16},{16,24},{1,9},{9,17},{17,25},{2,10},{10,18},{18,26},{... | collective-permute-start | bytes 1179656 | tf_op jit(solution)/shard_map/ppermute | solution.py:26
  358.4 21.7 %collective-permute-start.9 = (bf16[8,1,6,32,128]{4,3,2,1,0:T(8,128)(2,1)S(1)}, bf16[8,1,6,32,128]{4,3,2,1,0:T(8,128)(2,1)}, u32[]{:S(2)}, u32[]{:S(2)}) collective-permute-start(bf16[8,1,6,32,128]{4,3,2,1,0:T(8,128)(2,1)S(1)} %get-tuple-element.13), channel_id=1, source_target_pairs={{8,0},{16,8},{24,16},{9,1},{17,9},{25,17},{10,2},{18,10},{26,18},{... | collective-permute-start | bytes 1179656 | tf_op jit(solution)/shard_map/ppermute | solution.py:26
  380.1 2.5 copy-start.3
  382.1 1.7 copy-start.5
  382.1 6.2 %copy-start.22 = (bf16[2048,128,1,1,1,1,1]{0,1,6,5,4,3,2:T(8,128)(2,1)S(1)}, bf16[2048,128,1,1,1,1,1]{0,1,6,5,4,3,2:T(8,128)(2,1)}, u32[]{:S(2)}) copy-start(bf16[2048,128,1,1,1,1,1]{0,1,6,5,4,3,2:T(8,128)(2,1)} %copy-done.21) | copy-start | bytes 1572868
  382.6 8.1 %copy-start.4 = (bf16[8,8,6,32,128]{4,3,2,1,0:T(8,128)(2,1)}, bf16[8,8,6,32,128]{4,3,2,1,0:T(8,128)(2,1)S(1)}, u32[]{:S(2)}) copy-start(bf16[8,8,6,32,128]{4,3,2,1,0:T(8,128)(2,1)S(1)} %fusion.63) | copy-start | bytes 9437188
  383.9 144.2 %collective-permute-start.10 = (bf16[8,8,1,32,128]{4,3,2,1,0:T(8,128)(2,1)}, bf16[8,8,1,32,128]{4,3,2,1,0:T(8,128)(2,1)}, u32[]{:S(2)}, u32[]{:S(2)}) collective-permute-start(bf16[8,8,1,32,128]{4,3,2,1,0:T(8,128)(2,1)} %get-tuple-element.16), channel_id=1, source_target_pairs={{0,1},{1,2},{2,3},{3,4},{4,5},{5,6},{6,7},{8,9},{9,10},{10,11},{11... | collective-permute-start | bytes 1572872 | tf_op jit(solution)/shard_map/ppermute | solution.py:26
  386.8 141.2 %collective-permute-start.11 = (bf16[8,8,1,32,128]{4,3,2,1,0:T(8,128)(2,1)}, bf16[8,8,1,32,128]{4,3,2,1,0:T(8,128)(2,1)}, u32[]{:S(2)}, u32[]{:S(2)}) collective-permute-start(bf16[8,8,1,32,128]{4,3,2,1,0:T(8,128)(2,1)} %get-tuple-element.17), channel_id=1, source_target_pairs={{1,0},{2,1},{3,2},{4,3},{5,4},{6,5},{7,6},{9,8},{10,9},{11,10},{12... | collective-permute-start | bytes 1572872 | tf_op jit(solution)/shard_map/ppermute | solution.py:26
  524.6 6.7 %copy-start.1 = (f32[2048,256]{1,0:T(8,128)S(1)}, f32[2048,256]{1,0:T(8,128)}, u32[]{:S(2)}) copy-start(f32[2048,256]{1,0:T(8,128)} %param.9) | copy-start | bytes 6291460
  528.0 1.7 slice-start
Sparse Core Ops, SparseCore 0:
  121.4 145.5 all-reduce.2
  376.2 146.5 all-reduce.4
where the time goes:
time: 547 us; the launch traced here: 538 us
  waiting for transfers between devices  322 us (59%)
  matrix products  95.2 us (17%)
  starting transfers between devices  31.3 us (6%)
  blocking collectives  31 us (6%)
  other arithmetic  23.4 us (4%)
  local copies, waits for them, and re-layouts  20.5 us (4%)
  between operations  14.9 us (3%)
    psum x1, waiting for transfers between devices, body(): pre_one = lax.psum(partial_one, ('gx', 'gy', 'gz'))  145 us
    psum x1, waiting for transfers between devices, body(): grad_conv = lax.psum(kernel_local, ('gx', 'gy', 'gz')) / samples  123 us
    conv_general_dilated x1, matrix products, conv_back_input(): lax.conv_general_dilated(padded_grad, flipped, (1, 1, 1), 'VALID', dimens...  29.9 us
    ppermute x3, waiting for transfers between devices, with_halo(): after = lax.ppermute(initial, axis, down)  28.7 us
    conv_general_dilated x1, matrix products, conv_forward(): lax.conv_general_dilated(padded, kernel, (1, 1, 1), 'VALID', dimension_nu...  18.1 us
    all_to_all x1, blocking collectives, body(): lax.all_to_all(outgoing, ('gy', 'gz'), split_axis=0, concat_axis=4, tiled...  17.6 us
    conv_general_dilated x1, matrix products, conv_back_kernel(): lax.conv_general_dilated(padded, gradient, (1, 1, 1), 'VALID', dimension_...  15.5 us
    ppermute x6, starting transfers between devices, from_behind(): return lax.ppermute(block, axis, route)  13.9 us
  transfers between devices with their start and end apart: 14, of which 10 were waited for; matrix products, arithmetic and copies ran while one was open for 8% of the time, Pallas kernels for 0%

commit v1 on v0

--- a/solution.py
+++ b/solution.py
@@ -112,7 +112,9 @@
     partial_one = jnp.einsum(
         "uvxyzcb,xuyvzch->hb", arrived, weights_local, preferred_element_type=jnp.float32
     )
-    pre_one = lax.psum(partial_one, ("gx", "gy", "gz"))
+    pre_one = partial_one
+    for over in (("gy", "gz"), "gx"):
+        pre_one = lax.psum(pre_one, over)
     hidden_one = smooth_leaky(pre_one)
     pre_two = jnp.dot(dense_two.T, hidden_one, precision=lax.Precision.HIGHEST)
     hidden_two = smooth_leaky(pre_two)

time: 547 us -> 553 us (1.011)
    psum x1 -> x2, waiting for transfers between devices: 145 us -> 149 us  [body(): pre_one = lax.psum(pre_one, over)]
  transfers between devices with their start and end apart: 14 -> 15, of which waited for: 10 -> 11; matrix products, arithmetic and copies ran while one was open for 8% -> 8% of each run, Pallas kernels for 0% -> 0%
where the time goes in v1:
time: 553 us; the launch traced here: 545 us
  waiting for transfers between devices  325 us (59%)
  matrix products  95.2 us (17%)
  blocking collectives  34.4 us (6%)
  starting transfers between devices  31.7 us (6%)
  other arithmetic  23.4 us (4%)
  local copies, waits for them, and re-layouts  20.5 us (4%)
  between operations  14.6 us (3%)
    psum x2, waiting for transfers between devices, body(): pre_one = lax.psum(pre_one, over)  149 us
    psum x1, waiting for transfers between devices, body(): grad_conv = lax.psum(kernel_local, ('gx', 'gy', 'gz')) / samples  122 us
    conv_general_dilated x1, matrix products, conv_back_input(): lax.conv_general_dilated(padded_grad, flipped, (1, 1, 1), 'VALID', dimens...  29.9 us
    ppermute x3, waiting for transfers between devices, with_halo(): after = lax.ppermute(initial, axis, down)  28.7 us
    all_to_all x1, blocking collectives, body(): lax.all_to_all(outgoing, ('gy', 'gz'), split_axis=0, concat_axis=4, tiled...  20.9 us
    conv_general_dilated x1, matrix products, conv_forward(): lax.conv_general_dilated(padded, kernel, (1, 1, 1), 'VALID', dimension_nu...  18.1 us
    conv_general_dilated x1, matrix products, conv_back_kernel(): lax.conv_general_dilated(padded, gradient, (1, 1, 1), 'VALID', dimension_...  15.5 us
    ppermute x6, starting transfers between devices, from_behind(): return lax.ppermute(block, axis, route)  14.3 us
  transfers between devices with their start and end apart: 15, of which 11 were waited for; matrix products, arithmetic and copies ran while one was open for 8% of the time, Pallas kernels for 0%

profile of v1, /device:TPU:1, one launch (start us, length us, event | category | flops | bytes accessed | tf_op | source)
XLA Modules:
  0.0 545.1 jit_solution(5601406323933363507)
XLA Ops:
  7.2 1.2 fusion.69
  8.4 4.0 collective-permute-start
  12.5 1.3 collective-permute-start.1
  13.8 3.7 collective-permute-done
  17.5 2.4 constant_dynamic-update-slice_fusion.1
  19.9 1.4 collective-permute-done.1
  21.4 7.2 %collective-permute-start.2 = (bf16[10,1,4,32,128]{4,3,2,1,0:T(8,128)(2,1)S(1)}, bf16[10,1,4,32,128]{4,3,2,1,0:T(8,128)(2,1)S(1)}, u32[]{:S(2)}, u32[]{:S(2)}) collective-permute-start(bf16[10,1,4,32,128]{4,3,2,1,0:T(8,128)(2,1)S(1)} %get-tuple-element.18), channel_id=1, source_target_pairs={{0,8},{8,16},{16,24},{1,9},{9,17},{17,25},{2,10},{10,18},{18,26},{... | collective-permute-start | bytes 983048 | tf_op jit(solution)/shard_map/ppermute | solution.py:17
  28.6 1.9 collective-permute-start.3
  30.5 2.1 collective-permute-done.2
  32.6 23.5 %collective-permute-done.3 = bf16[10,1,4,32,128]{4,3,2,1,0:T(8,128)(2,1)S(1)} collective-permute-done((bf16[10,1,4,32,128]{4,3,2,1,0:T(8,128)(2,1)S(1)}, bf16[10,1,4,32,128]{4,3,2,1,0:T(8,128)(2,1)S(1)}, u32[]{:S(2)}, u32[]{:S(2)}) %collective-permute-start.3) | collective-permute-done | bytes 327712 | tf_op jit(solution)/shard_map/ppermute | solution.py:18
  56.3 1.3 collective-permute-start.4
  57.6 1.3 collective-permute-start.5
  58.9 7.9 %collective-permute-done.4 = bf16[10,10,1,32,128]{4,3,2,1,0:T(8,128)(2,1)S(1)} collective-permute-done((bf16[10,10,1,32,128]{4,3,2,1,0:T(8,128)(2,1)S(1)}, bf16[10,10,1,32,128]{4,3,2,1,0:T(8,128)(2,1)S(1)}, u32[]{:S(2)}, u32[]{:S(2)}) %collective-permute-start.4) | collective-permute-done | bytes 819232 | tf_op jit(solution)/shard_map/ppermute | solution.py:17
  66.8 3.9 collective-permute-done.5
  70.7 18.1 %fusion.2 = (f32[8,8,4,64,128]{4,3,2,1,0:T(8,128)}, f32[8,8,4,64,128]{4,3,2,1,0:T(8,128)}) fusion(bf16[3,3,3,32,64]{4,3,2,1,0:T(8,128)(2,1)S(1)} %copy-done.12, bf16[10,10,1,32,128]{4,3,2,1,0:T(8,128)(2,1)S(1)} %collective-permute-done.5, bf16[10,1,4,32,128]{4,3,2,1,0:T(8,128)(2,1)S(1)} %collective-permute-done.3, ...), kind=kOutput, calls=%fused_computation.4 | convolution fusion | flops 3652583424 | bytes 21803008 | tf_op jit(solution)/shard_map/conv_general_dilated | solution.py:42
  88.8 4.4 reduce_sum.9
  93.9 13.4 %all_to_all.24 = bf16[1,4,4,2,64,128]{5,3,2,1,0,4:T(2,128)(2,1)S(1)} all-to-all(bf16[1,4,4,2,64,128]{5,3,2,1,0,4:T(2,128)(2,1)S(1)} %copy.45), channel_id=1, replica_groups=mesh['gx'=4,'gy'=4,'gz'=8] {'gy','gz'}, dimensions={4} | all-to-all | bytes 1048576 | tf_op jit(solution)/shard_map/all_to_all | solution.py:107
  107.5 13.7 %fusion.7 = f32[2048,128]{0,1:T(8,128)} fusion(bf16[4,4,4,8,2,2,2048]{6,5,4,3,2,1,0:T(2,128)(2,1)} %bitcast.72, bf16[32,1,4,4,2,2,128]{6,5,0,4,3,2,1:T(2,128)(2,1)S(1)} %bitcast.70), kind=kOutput, calls=%fused_computation.14 | convolution fusion | flops 1073741824 | bytes 9961472 | tf_op jit(solution)/shard_map/uvxyzcb,xuyvzch->hb/dot_general | solution.py:112
  121.4 103.0 %all-reduce.4.cloned.1.call-done = f32[2048,128]{0,1:T(8,128)} async-done(((f32[2048,128]{0,1:T(8,128)}), f32[2048,128]{0,1:T(8,128)}) %all-reduce.4.cloned.1.call-update) | async-done | bytes 1048592 | tf_op jit(solution)/shard_map/psum | solution.py:117
  224.6 45.9 %all-reduce.6.cloned.1.call-done = f32[2048,128]{0,1:T(8,128)} async-done(((f32[2048,128]{0,1:T(8,128)}), f32[2048,128]{0,1:T(8,128)}) %all-reduce.6.cloned.1.call-update) | async-done | bytes 1048592 | tf_op jit(solution)/shard_map/psum | solution.py:117
  270.5 3.0 convolution_bitcast_fusion.2
  274.1 3.5 fusion.12
  277.7 8.6 %fusion.16 = bf16[4,8,4,4,2,2,128]{6,1,5,4,3,0,2:T(8,128)(2,1)S(1)} fusion(bf16[2048,128,1,1,1,1,1]{0,1,6,5,4,3,2:T(8,128)(2,1)S(1)} %fusion.12, bf16[4,4,4,8,2,2,2048]{6,5,4,3,2,1,0:T(2,128)(2,1)} %bitcast.73), kind=kOutput, calls=%fused_computation.21 | convolution fusion | flops 1074003968 | bytes 9437184 | tf_op jit(solution)/shard_map/xuyvzch,hb->uvxyzcb/dot_general | solution.py:134
  287.0 20.9 %all_to_all.25 = bf16[32,4,4,2,2,128]{5,4,3,2,1,0:T(2,128)(2,1)S(1)} all-to-all(bf16[32,4,4,2,2,128]{5,4,3,2,1,0:T(2,128)(2,1)S(1)} %copy.56), channel_id=1, replica_groups=mesh['gx'=4,'gy'=4,'gz'=8] {'gy','gz'}, dimensions={0} | all-to-all | bytes 1048576 | tf_op jit(solution)/shard_map/all_to_all | solution.py:138
  309.1 1.1 broadcast_in_dim.2
  310.2 1.1 slice-done.2
  311.3 2.8 multiply_convert_fusion.1
  314.1 29.9 %fusion.70 = (bf16[10,10,6,32,128]{4,3,2,1,0:T(8,128)(2,1)S(1)}, f32[10,10,6,32,128]{4,3,2,1,0:T(8,128)S(1)}) fusion(bf16[8,8,4,64,128]{4,3,2,1,0:T(8,128)(2,1)S(1)} %multiply_convert_fusion.1, bf16[3,3,3,32,64]{4,3,2,1,0:T(8,128)(2,1)S(1)} %copy-done.13), kind=kOutput, calls=%fused_computation.92 | convolution fusion | flops 3626336256 | bytes 19050496 | tf_op jit(solution)/shard_map/conv_general_dilated | solution.py:54
  344.1 2.5 collective-permute-start.6
  346.6 1.3 collective-permute-start.7
  347.9 1.2 slice.107
  349.1 7.6 %collective-permute-done.6 = bf16[1,10,6,32,128]{4,3,2,1,0:T(8,128)(2,1)S(1)} collective-permute-done((bf16[1,10,6,32,128]{4,3,2,1,0:T(8,128)(2,1)S(1)}, bf16[1,10,6,32,128]{4,3,2,1,0:T(8,128)(2,1)S(1)}, u32[]{:S(2)}, u32[]{:S(2)}) %collective-permute-start.6) | collective-permute-done | bytes 491552 | tf_op jit(solution)/shard_map/ppermute | solution.py:26
  356.7 4.0 collective-permute-done.7
  361.8 3.9 collective-permute-start.8
  365.7 2.1 collective-permute-start.9
  367.8 15.5 %fusion.61 = f32[3,3,3,32,64]{4,3,2,1,0:T(8,128)} fusion(bf16[8,8,4,64,128]{4,3,2,1,0:T(8,128)(2,1)S(1)} %multiply_convert_fusion.1, bf16[10,10,1,32,128]{4,3,2,1,0:T(8,128)(2,1)S(1)} %copy-done.17, bf16[10,1,4,32,128]{4,3,2,1,0:T(8,128)(2,1)S(1)} %copy-done.11, bf16[10,8,4,32,128]{4,3,2,1,0:T(8,128)(2,1)S(1)} %copy-done.7, ...), kind=kOutput, calls=%fused_computation.83 | convolution fusion | flops 3633709056 | bytes 9330688 | tf_op jit(solution)/shard_map/conv_general_dilated | solution.py:65
  383.3 3.5 pad_maximum_fusion
  387.4 2.0 slice_add_fusion.5
  389.9 1.2 fusion.67
  391.1 3.0 collective-permute-start.10
  394.1 1.5 collective-permute-start.11
  395.6 2.3 fusion
  398.0 9.4 %copy.52 = bf16[4,4,4,8,2,2,2048]{6,5,4,3,2,1,0:T(2,128)(2,1)} copy(bf16[4,4,4,8,2,2,2048]{6,3,5,4,2,0,1:T(8,128)(2,1)S(1)} %fusion) | data formatting | bytes 16777216 | tf_op jit(solution)/shard_map/convert_element_type | solution.py:133
  407.3 122.5 %all-reduce.8.cloned.1.call-done = f32[3,3,3,32,64]{4,3,2,1,0:T(8,128)} async-done(((f32[3,3,3,32,64]{4,3,2,1,0:T(8,128)}), f32[3,3,3,32,64]{4,3,2,1,0:T(8,128)}) %all-reduce.8.cloned.1.call-update) | async-done | bytes 221200 | tf_op jit(solution)/shard_map/psum | solution.py:156
  529.8 1.8 broadcast_multiply_fusion
  531.6 3.4 pad_maximum_fusion.1
  535.1 1.7 fusion.24
  536.8 1.5 pad_maximum_fusion.3
  (81 shorter events, 6.2 us)
Async XLA Ops:
  7.2 263.3 %copy-start = (f32[2048,256]{1,0:T(8,128)S(1)}, f32[2048,256]{1,0:T(8,128)}, u32[]{:S(2)}) copy-start(f32[2048,256]{1,0:T(8,128)} %param.9) | copy-start | bytes 6291460
  7.2 217.1 %all-reduce.4.cloned.1.call-start = ((), (), s32[]{:S(2)}) async-start(), calls=%async_computation.2 | async-start | bytes 2097152 | tf_op jit(solution)/shard_map/psum | solution.py:117
  8.4 9.0 %collective-permute-start = (bf16[1,8,4,32,128]{4,3,2,1,0:T(8,128)(2,1)S(1)}, bf16[1,8,4,32,128]{4,3,2,1,0:T(8,128)(2,1)S(1)}, u32[]{:S(2)}, u32[]{:S(2)}) collective-permute-start(bf16[1,8,4,32,128]{4,3,2,1,0:T(8,128)(2,1)S(1)} %get-tuple-element.21), channel_id=1, source_target_pairs={{0,32},{32,64},{64,96},{1,33},{33,65},{65,97},{2,34},{34,66},{66,9... | collective-permute-start | bytes 786440 | tf_op jit(solution)/shard_map/ppermute | solution.py:17
  12.5 8.8 %collective-permute-start.1 = (bf16[1,8,4,32,128]{4,3,2,1,0:T(8,128)(2,1)S(1)}, bf16[1,8,4,32,128]{4,3,2,1,0:T(8,128)(2,1)S(1)}, u32[]{:S(2)}, u32[]{:S(2)}) collective-permute-start(bf16[1,8,4,32,128]{4,3,2,1,0:T(8,128)(2,1)S(1)} %get-tuple-element.20), channel_id=1, source_target_pairs={{32,0},{64,32},{96,64},{33,1},{65,33},{97,65},{34,2},{66,34},{98,6... | collective-permute-start | bytes 786440 | tf_op jit(solution)/shard_map/ppermute | solution.py:18
  17.5 53.2 %copy-start.12 = (bf16[3,3,3,32,64]{4,3,2,1,0:T(8,128)(2,1)S(1)}, bf16[3,3,3,32,64]{4,3,2,1,0:T(8,128)(2,1)}, u32[]{:S(2)}) copy-start(bf16[3,3,3,32,64]{4,3,2,1,0:T(8,128)(2,1)} %param.7) | copy-start | bytes 331780
  21.3 67.4 %copy-start.6 = (bf16[10,8,4,32,128]{4,3,2,1,0:T(8,128)(2,1)}, bf16[10,8,4,32,128]{4,3,2,1,0:T(8,128)(2,1)S(1)}, u32[]{:S(2)}) copy-start(bf16[10,8,4,32,128]{4,3,2,1,0:T(8,128)(2,1)S(1)} %constant_dynamic-update-slice_fusion) | copy-start | bytes 7864324
  21.4 11.2 %collective-permute-start.2 = (bf16[10,1,4,32,128]{4,3,2,1,0:T(8,128)(2,1)S(1)}, bf16[10,1,4,32,128]{4,3,2,1,0:T(8,128)(2,1)S(1)}, u32[]{:S(2)}, u32[]{:S(2)}) collective-permute-start(bf16[10,1,4,32,128]{4,3,2,1,0:T(8,128)(2,1)S(1)} %get-tuple-element.18), channel_id=1, source_target_pairs={{0,8},{8,16},{16,24},{1,9},{9,17},{17,25},{2,10},{10,18},{18,26},{... | collective-permute-start | bytes 983048 | tf_op jit(solution)/shard_map/ppermute | solution.py:17
  28.6 27.5 %collective-permute-start.3 = (bf16[10,1,4,32,128]{4,3,2,1,0:T(8,128)(2,1)S(1)}, bf16[10,1,4,32,128]{4,3,2,1,0:T(8,128)(2,1)S(1)}, u32[]{:S(2)}, u32[]{:S(2)}) collective-permute-start(bf16[10,1,4,32,128]{4,3,2,1,0:T(8,128)(2,1)S(1)} %get-tuple-element.19), channel_id=1, source_target_pairs={{8,0},{16,8},{24,16},{9,1},{17,9},{25,17},{10,2},{18,10},{26,18},{... | collective-permute-start | bytes 983048 | tf_op jit(solution)/shard_map/ppermute | solution.py:18
  32.6 56.2 %copy-start.8 = (bf16[10,1,4,32,128]{4,3,2,1,0:T(8,128)(2,1)}, bf16[10,1,4,32,128]{4,3,2,1,0:T(8,128)(2,1)S(1)}, u32[]{:S(2)}) copy-start(bf16[10,1,4,32,128]{4,3,2,1,0:T(8,128)(2,1)S(1)} %collective-permute-done.2) | copy-start | bytes 983044
  56.1 32.7 %copy-start.10 = (bf16[10,1,4,32,128]{4,3,2,1,0:T(8,128)(2,1)}, bf16[10,1,4,32,128]{4,3,2,1,0:T(8,128)(2,1)S(1)}, u32[]{:S(2)}) copy-start(bf16[10,1,4,32,128]{4,3,2,1,0:T(8,128)(2,1)S(1)} %collective-permute-done.3) | copy-start | bytes 983044
  56.3 10.6 %collective-permute-start.4 = (bf16[10,10,1,32,128]{4,3,2,1,0:T(8,128)(2,1)S(1)}, bf16[10,10,1,32,128]{4,3,2,1,0:T(8,128)(2,1)S(1)}, u32[]{:S(2)}, u32[]{:S(2)}) collective-permute-start(bf16[10,10,1,32,128]{4,3,2,1,0:T(8,128)(2,1)S(1)} %get-tuple-element.14), channel_id=1, source_target_pairs={{0,1},{1,2},{2,3},{3,4},{4,5},{5,6},{6,7},{8,9},{9,10},{10,11},{11... | collective-permute-start | bytes 2457608 | tf_op jit(solution)/shard_map/ppermute | solution.py:17
  57.6 13.1 %collective-permute-start.5 = (bf16[10,10,1,32,128]{4,3,2,1,0:T(8,128)(2,1)S(1)}, bf16[10,10,1,32,128]{4,3,2,1,0:T(8,128)(2,1)S(1)}, u32[]{:S(2)}, u32[]{:S(2)}) collective-permute-start(bf16[10,10,1,32,128]{4,3,2,1,0:T(8,128)(2,1)S(1)} %get-tuple-element.15), channel_id=1, source_target_pairs={{1,0},{2,1},{3,2},{4,3},{5,4},{6,5},{7,6},{9,8},{10,9},{11,10},{12... | collective-permute-start | bytes 2457608 | tf_op jit(solution)/shard_map/ppermute | solution.py:18
  66.8 22.0 %copy-start.14 = (bf16[10,10,1,32,128]{4,3,2,1,0:T(8,128)(2,1)}, bf16[10,10,1,32,128]{4,3,2,1,0:T(8,128)(2,1)S(1)}, u32[]{:S(2)}) copy-start(bf16[10,10,1,32,128]{4,3,2,1,0:T(8,128)(2,1)S(1)} %collective-permute-done.4) | copy-start | bytes 2457604
  70.7 18.1 %copy-start.16 = (bf16[10,10,1,32,128]{4,3,2,1,0:T(8,128)(2,1)}, bf16[10,10,1,32,128]{4,3,2,1,0:T(8,128)(2,1)S(1)}, u32[]{:S(2)}) copy-start(bf16[10,10,1,32,128]{4,3,2,1,0:T(8,128)(2,1)S(1)} %collective-permute-done.5) | copy-start | bytes 2457604
  121.3 152.2 %copy-start.18 = (f32[256,4]{0,1:T(4,128)S(1)}, f32[256,4]{0,1:T(4,128)}, u32[]{:S(2)}) copy-start(f32[256,4]{0,1:T(4,128)} %param.10) | copy-start | bytes 12292
  121.3 152.5 %copy-start.19 = (f32[4,128]{1,0:T(4,128)S(1)}, f32[4,128]{1,0:T(4,128)}, u32[]{:S(2)}) copy-start(f32[4,128]{1,0:T(4,128)} %param.11) | copy-start | bytes 6148
  121.3 149.2 %all-reduce.6.cloned.1.call-start = ((), (), s32[]{:S(2)}) async-start(), calls=%async_computation.3 | async-start | bytes 2097152 | tf_op jit(solution)/shard_map/psum | solution.py:117
  224.3 305.5 %all-reduce.8.cloned.1.call-start = ((), (), s32[]{:S(2)}) async-start(), calls=%async_computation.4 | async-start | bytes 884736 | tf_op jit(solution)/shard_map/psum | solution.py:156
  273.7 12.5 %copy-start.20 = (f32[4,128]{1,0:T(4,128)}, f32[4,128]{1,0:T(4,128)S(1)}, u32[]{:S(2)}) copy-start(f32[4,128]{1,0:T(4,128)S(1)} %convolution_bitcast_fusion.3) | copy-start | bytes 6148
  277.7 8.6 %copy-start.21 = (bf16[2048,128,1,1,1,1,1]{0,1,6,5,4,3,2:T(8,128)(2,1)}, bf16[2048,128,1,1,1,1,1]{0,1,6,5,4,3,2:T(8,128)(2,1)S(1)}, u32[]{:S(2)}) copy-start(bf16[2048,128,1,1,1,1,1]{0,1,6,5,4,3,2:T(8,128)(2,1)S(1)} %fusion.12) | copy-start | bytes 1572868
  286.5 23.7 %slice-start.1 = ((s8[8388608]{0:T(1024)(128)(4,1)}), s8[4194304]{0:T(1024)(128)(4,1)S(1)}, s32[]{:S(2)}) async-start(s8[8388608]{0:T(1024)(128)(4,1)} %bitcast.65), calls=%async_computation.6 | async-start | bytes 8388608
  309.1 2.2 slice-start.2
  311.3 2.8 copy-start.13
  344.1 12.6 %collective-permute-start.6 = (bf16[1,10,6,32,128]{4,3,2,1,0:T(8,128)(2,1)S(1)}, bf16[1,10,6,32,128]{4,3,2,1,0:T(8,128)(2,1)S(1)}, u32[]{:S(2)}, u32[]{:S(2)}) collective-permute-start(bf16[1,10,6,32,128]{4,3,2,1,0:T(8,128)(2,1)S(1)} %get-tuple-element.10), channel_id=1, source_target_pairs={{0,32},{32,64},{64,96},{1,33},{33,65},{65,97},{2,34},{34,66},{66,9... | collective-permute-start | bytes 1474568 | tf_op jit(solution)/shard_map/ppermute | solution.py:26
  346.6 14.1 %collective-permute-start.7 = (bf16[1,10,6,32,128]{4,3,2,1,0:T(8,128)(2,1)S(1)}, bf16[1,10,6,32,128]{4,3,2,1,0:T(8,128)(2,1)S(1)}, u32[]{:S(2)}, u32[]{:S(2)}) collective-permute-start(bf16[1,10,6,32,128]{4,3,2,1,0:T(8,128)(2,1)S(1)} %get-tuple-element.11), channel_id=1, source_target_pairs={{32,0},{64,32},{96,64},{33,1},{65,33},{97,65},{34,2},{66,34},{98,6... | collective-permute-start | bytes 1474568 | tf_op jit(solution)/shard_map/ppermute | solution.py:26
  349.1 12.6 %copy-start.2 = (f32[6,10,6,32,128]{4,3,2,1,0:T(8,128)}, f32[6,10,6,32,128]{4,3,2,1,0:T(8,128)S(1)}, u32[]{:S(2)}) copy-start(f32[6,10,6,32,128]{4,3,2,1,0:T(8,128)S(1)} %slice.107) | copy-start | bytes 17694724
  361.0 6.8 %copy-start.7 = (bf16[10,8,4,32,128]{4,3,2,1,0:T(8,128)(2,1)S(1)}, bf16[10,8,4,32,128]{4,3,2,1,0:T(8,128)(2,1)}, u32[]{:S(2)}) copy-start(bf16[10,8,4,32,128]{4,3,2,1,0:T(8,128)(2,1)} %copy-done.6) | copy-start | bytes 7864324
  361.0 6.8 %copy-start.9 = (bf16[10,1,4,32,128]{4,3,2,1,0:T(8,128)(2,1)S(1)}, bf16[10,1,4,32,128]{4,3,2,1,0:T(8,128)(2,1)}, u32[]{:S(2)}) copy-start(bf16[10,1,4,32,128]{4,3,2,1,0:T(8,128)(2,1)} %copy-done.8) | copy-start | bytes 983044
  361.0 6.8 %copy-start.11 = (bf16[10,1,4,32,128]{4,3,2,1,0:T(8,128)(2,1)S(1)}, bf16[10,1,4,32,128]{4,3,2,1,0:T(8,128)(2,1)}, u32[]{:S(2)}) copy-start(bf16[10,1,4,32,128]{4,3,2,1,0:T(8,128)(2,1)} %copy-done.10) | copy-start | bytes 983044
  361.0 6.8 %copy-start.15 = (bf16[10,10,1,32,128]{4,3,2,1,0:T(8,128)(2,1)S(1)}, bf16[10,10,1,32,128]{4,3,2,1,0:T(8,128)(2,1)}, u32[]{:S(2)}) copy-start(bf16[10,10,1,32,128]{4,3,2,1,0:T(8,128)(2,1)} %copy-done.14) | copy-start | bytes 2457604
  361.0 6.8 %copy-start.17 = (bf16[10,10,1,32,128]{4,3,2,1,0:T(8,128)(2,1)S(1)}, bf16[10,10,1,32,128]{4,3,2,1,0:T(8,128)(2,1)}, u32[]{:S(2)}) copy-start(bf16[10,10,1,32,128]{4,3,2,1,0:T(8,128)(2,1)} %copy-done.16) | copy-start | bytes 2457604
  361.8 25.6 %collective-permute-start.8 = (bf16[8,1,6,32,128]{4,3,2,1,0:T(8,128)(2,1)S(1)}, bf16[8,1,6,32,128]{4,3,2,1,0:T(8,128)(2,1)}, u32[]{:S(2)}, u32[]{:S(2)}) collective-permute-start(bf16[8,1,6,32,128]{4,3,2,1,0:T(8,128)(2,1)S(1)} %get-tuple-element.12), channel_id=1, source_target_pairs={{0,8},{8,16},{16,24},{1,9},{9,17},{17,25},{2,10},{10,18},{18,26},{... | collective-permute-start | bytes 1179656 | tf_op jit(solution)/shard_map/ppermute | solution.py:26
  365.7 21.7 %collective-permute-start.9 = (bf16[8,1,6,32,128]{4,3,2,1,0:T(8,128)(2,1)S(1)}, bf16[8,1,6,32,128]{4,3,2,1,0:T(8,128)(2,1)}, u32[]{:S(2)}, u32[]{:S(2)}) collective-permute-start(bf16[8,1,6,32,128]{4,3,2,1,0:T(8,128)(2,1)S(1)} %get-tuple-element.13), channel_id=1, source_target_pairs={{8,0},{16,8},{24,16},{9,1},{17,9},{25,17},{10,2},{18,10},{26,18},{... | collective-permute-start | bytes 1179656 | tf_op jit(solution)/shard_map/ppermute | solution.py:26
  387.4 2.5 copy-start.3
  389.4 1.7 copy-start.5
  389.4 6.2 %copy-start.22 = (bf16[2048,128,1,1,1,1,1]{0,1,6,5,4,3,2:T(8,128)(2,1)S(1)}, bf16[2048,128,1,1,1,1,1]{0,1,6,5,4,3,2:T(8,128)(2,1)}, u32[]{:S(2)}) copy-start(bf16[2048,128,1,1,1,1,1]{0,1,6,5,4,3,2:T(8,128)(2,1)} %copy-done.21) | copy-start | bytes 1572868
  389.9 8.1 %copy-start.4 = (bf16[8,8,6,32,128]{4,3,2,1,0:T(8,128)(2,1)}, bf16[8,8,6,32,128]{4,3,2,1,0:T(8,128)(2,1)S(1)}, u32[]{:S(2)}) copy-start(bf16[8,8,6,32,128]{4,3,2,1,0:T(8,128)(2,1)S(1)} %fusion.63) | copy-start | bytes 9437188
  391.1 144.0 %collective-permute-start.10 = (bf16[8,8,1,32,128]{4,3,2,1,0:T(8,128)(2,1)}, bf16[8,8,1,32,128]{4,3,2,1,0:T(8,128)(2,1)}, u32[]{:S(2)}, u32[]{:S(2)}) collective-permute-start(bf16[8,8,1,32,128]{4,3,2,1,0:T(8,128)(2,1)} %get-tuple-element.16), channel_id=1, source_target_pairs={{0,1},{1,2},{2,3},{3,4},{4,5},{5,6},{6,7},{8,9},{9,10},{10,11},{11... | collective-permute-start | bytes 1572872 | tf_op jit(solution)/shard_map/ppermute | solution.py:26
  394.1 141.0 %collective-permute-start.11 = (bf16[8,8,1,32,128]{4,3,2,1,0:T(8,128)(2,1)}, bf16[8,8,1,32,128]{4,3,2,1,0:T(8,128)(2,1)}, u32[]{:S(2)}, u32[]{:S(2)}) collective-permute-start(bf16[8,8,1,32,128]{4,3,2,1,0:T(8,128)(2,1)} %get-tuple-element.17), channel_id=1, source_target_pairs={{1,0},{2,1},{3,2},{4,3},{5,4},{6,5},{7,6},{9,8},{10,9},{11,10},{12... | collective-permute-start | bytes 1572872 | tf_op jit(solution)/shard_map/ppermute | solution.py:26
  531.6 6.7 %copy-start.1 = (f32[2048,256]{1,0:T(8,128)S(1)}, f32[2048,256]{1,0:T(8,128)}, u32[]{:S(2)}) copy-start(f32[2048,256]{1,0:T(8,128)} %param.9) | copy-start | bytes 6291460
  535.1 1.7 slice-start
Sparse Core Ops, SparseCore 0:
  121.4 102.8 all-reduce.3
  226.7 43.7 all-reduce.5
  383.4 146.3 all-reduce.7
